TPU v7x, 64 devices: a 2x2x8 block of a 4x4x8 slice. The times are simulated.
64 devices in a mesh: dp: 8 (over x, y, core), sp: 8 (over z).
Axes of the slice: x: 2, y: 2, z: 8, core: 2. Of those that a mesh axis runs over, the one named last changes fastest.
The devices are a block of a 4x4x8 slice.
Arguments:
- q: bfloat16 [256, 24, 128], P('dp'), parts along dimension 0
- k: bfloat16 [256, 4096, 8, 128], P('dp', 'sp'), parts along dimension 0
- v: bfloat16 [256, 4096, 8, 128], P('dp', 'sp'), parts along dimension 0
Outputs:
- q: bfloat16 [256, 24, 128], P('dp'), parts along dimension 0
There are 8 independent parts. A program takes and returns all parts, laid end to end along the dimension named above; each array names one.
All inputs are finite; a program needn't handle non-finite values.
Results may differ from a plain program's by a relative error of at most 0.012.
Values are sent between devices in bfloat16 or wider.
A program may use at most 768 MiB of HBM per device.

v0:
```python
import jax
import jax.numpy as jnp
from jax import lax
from jax.sharding import PartitionSpec as P


def einsum(form, a, b):
    return jnp.einsum(form, a.astype(jnp.float32), b.astype(jnp.float32))


def part_of(q, k, v):
    grouped = q.reshape(q.shape[0], k.shape[2], -1, q.shape[2])
    scores = einsum("bgsd,bugd->bgsu", grouped, k) * q.shape[2] ** -0.5
    high = jnp.max(scores, -1, keepdims=True)
    weights = jnp.exp(scores - high)
    seen = einsum("bgsu,bugd->bgsd", weights.astype(jnp.bfloat16), v)
    return jnp.concatenate([seen, jnp.sum(weights, -1, keepdims=True), high], -1)


def together(parts):
    seen, total, high = parts[..., :-2], parts[..., -2:-1], parts[..., -1:]
    scale = jnp.exp(high - jnp.max(high, 0))
    return (jnp.sum(seen * scale, 0) / jnp.sum(total * scale, 0)).astype(jnp.bfloat16)


def solution(mesh):
    def step(q, k, v):
        return together(lax.all_gather(part_of(q, k, v), "sp")).reshape(q.shape)

    return jax.shard_map(
        step,
        mesh=mesh,
        in_specs=(P("dp", None, None), P("dp", "sp", None, None), P("dp", "sp", None, None)),
        out_specs=P("dp", None, None),
        check_vma=False,
    )
```

profile of v0, /device:TPU:21, one launch (start us, length us, event | category | flops | bytes accessed | tf_op | source)
XLA Modules:
  0.0 139.2 jit_solution(1916560967131067477)
XLA Ops:
  6.5 0.0 all-gather.3.cloned.1.call-start
  6.6 1.0 copy.46
  7.5 14.3 %multiply_reduce_fusion = (f32[32,8,3]{2,1,0:T(8,128)S(1)}, f32[32,8,3,512]{3,2,1,0:T(4,128)S(1)}) fusion(bf16[32,512,8,128]{3,2,1,0:T(8,128)(2,1)} %param.4, bf16[32,8,3,128]{3,0,2,1:T(8,128)(2,1)S(1)} %bitcast.14), kind=kOutput, calls=%fused_computation.7 | convolution fusion | flops 101448960 | bytes 35326976 | tf_op jit(solution)/shard_map/bgsd,bugd->bgsu/dot_general | solution.py:8
  21.9 1.2 fusion.5
  23.0 15.1 %fusion = f32[32,8,3,128]{3,2,1,0:T(4,128)S(1)} fusion(bf16[32,512,8,128]{3,2,1,0:T(8,128)(2,1)} %param.5, f32[32,8,3,512]{3,2,1,0:T(4,128)S(1)} %get-tuple-element.11, f32[32,8,3]{2,1,0:T(8,128)S(1)} %get-tuple-element.10), kind=kOutput, calls=%fused_computation | convolution fusion | flops 101842944 | bytes 35523584 | tf_op jit(solution)/shard_map/bgsu,bugd->bgsd/dot_general | solution.py:8
  38.1 1.7 %copy.52 = f32[32,8,3,1]{3,2,1,0:T(4,128)S(1)} copy(f32[32,8,3,1]{2,1,0,3:T(8,128)S(1)} %bitcast.16) | data formatting | bytes 6144 | tf_op jit(solution)/shard_map/broadcast_in_dim | solution.py:17
  39.8 1.7 %copy.53 = f32[32,8,3,1]{3,2,1,0:T(4,128)S(1)} copy(f32[32,8,3,1]{2,1,0,3:T(8,128)S(1)} %bitcast.15) | data formatting | bytes 6144 | tf_op jit(solution)/shard_map/broadcast_in_dim | solution.py:14
  41.4 0.4 pad_maximum_fusion
  41.8 1.0 copy.54
  42.9 0.1 all-gather.3.cloned.1.call-update
  42.9 75.6 %all-gather.3.cloned.1.call-done = f32[256,8,3,130]{3,1,2,0:T(8,128)} async-done(((f32[32,8,3,130]{3,1,2,0:T(8,128)}), f32[256,8,3,130]{3,1,2,0:T(8,128)}) %all-gather.3.cloned.1.call-update) | async-done | bytes 3194896 | tf_op jit(solution)/shard_map/all_gather | solution.py:28
  118.5 5.7 %fusion.14 = (f32[8,32,8,3,1]{4,2,3,1,0:T(8,128)}, f32[32,8,3]{1,2,0:T(4,128)S(1)}, f32[8,32,8,3,1]{4,2,3,1,0:T(8,128)S(1)}) fusion(f32[8,32,8,3,130]{4,2,3,1,0:T(8,128)} %bitcast.12), kind=kLoop, calls=%fused_computation.21 | loop fusion | flops 5376 | bytes 101376 | tf_op jit(solution)/shard_map/slice | solution.py:21
  124.3 2.7 %copy.68 = f32[8,32,8,3,1]{1,2,4,3,0:T(8,128)S(1)} copy(f32[8,32,8,3,1]{4,2,3,1,0:T(8,128)} %get-tuple-element.5) | data formatting | bytes 49152
  126.9 0.1 copy.70
  127.0 1.5 %copy.67 = f32[8,32,8,3,1]{1,2,4,3,0:T(8,128)S(1)} copy(f32[8,32,8,3,1]{4,2,3,1,0:T(8,128)S(1)} %get-tuple-element.7) | data formatting | bytes 49152
  128.6 0.2 copy.56
  128.8 2.5 %fusion.4 = f32[32,8,3,128]{3,1,2,0:T(8,128)S(1)} fusion(f32[8,32,8,3,130]{4,2,3,1,0:T(8,128)} %bitcast.13, f32[8,32,8,3]{2,3,1,0:T(4,128)S(1)} %copy.56), kind=kLoop, calls=%fused_computation.5 | loop fusion | flops 1474560 | bytes 3563520 | tf_op jit(solution)/shard_map/reduce_sum | solution.py:23
  131.3 0.1 copy.58
  131.4 0.2 fusion.10
  131.6 0.8 copy.61
  (3 shorter events, 0.1 us)
Async XLA Ops:
  6.5 112.0 %all-gather.3.cloned.1.call-start = ((), (), s32[]{:S(2)}) async-start(), calls=%async_computation | async-start | bytes 7077888 | tf_op jit(solution)/shard_map/all_gather | solution.py:28
Sparse Core Ops, SparseCore 0:
  43.1 75.4 all-gather.2
where the time goes:
time: 139 us
  waiting for transfers between devices  75.6 us (54%)
  matrix products  29.4 us (21%)
  between operations  13.5 us (10%)
  local copies, waits for them, and re-layouts  10.7 us (8%)
  other arithmetic  9.99 us (7%)
    all_gather x1, waiting for transfers between devices, step(): return together(lax.all_gather(part_of(q, k, v), 'sp')).reshape(q.shape)  75.6 us
    dot_general x2, matrix products, einsum(): return jnp.einsum(form, a.astype(jnp.float32), b.astype(jnp.float32))  29.4 us
    slice x1, other arithmetic, together(): seen, total, high = (parts[..., :-2], parts[..., -2:-1], parts[..., -1:])  5.73 us
    unnamed x4, local copies, waits for them, and re-layouts  5.2 us
  transfers between devices with their start and end apart: 1, of which 1 were waited for; matrix products, arithmetic and copies ran while one was open for 0% of the time, Pallas kernels for 0%

commit v1 on v0

v1 whole, which is shorter than its diff:
```python
import functools
import math

import jax
import jax.numpy as jnp
from jax import lax
from jax.experimental import pallas as pl
from jax.experimental.pallas import tpu as pltpu
from jax.sharding import PartitionSpec as P

LANES = 128
SIDE = 256
SLOTS = 8
SUMS = 32


def attend(q_ref, k_hbm, v_hbm, out_ref, kbuf, vbuf, scores, highs, part, stat, parts, stats,
           k_sem, v_sem, part_out, stat_out, part_in, stat_in, res_out, res_in, *, n, heads_per):
    batch, heads, head = q_ref.shape
    rows = k_hbm.shape[1]
    tiles = rows // (2 * SIDE)
    key_heads = heads // heads_per
    rounds = batch // n
    factor = head**-0.5 * math.log2(math.e)
    me = lax.axis_index("sp")

    def seq_of(p):
        step = p % n
        half = (step + 1) // 2
        return (p // n) * n + (me + n // 2 + (1 - 2 * (step % 2)) * half + n) % n

    def owner_of(p):
        step = p % n
        half = (step + 1) // 2
        return (me + n // 2 + (1 - 2 * (step % 2)) * half + n) % n

    def fetch_k(p):
        return pltpu.make_async_copy(k_hbm.at[seq_of(p)], kbuf.at[p % SLOTS], k_sem.at[p % SLOTS])

    def fetch_v(p):
        return pltpu.make_async_copy(v_hbm.at[seq_of(p)], vbuf.at[p % SLOTS], v_sem.at[p % SLOTS])

    barrier = pltpu.get_barrier_semaphore()
    for hop in range(1, n):
        pl.semaphore_signal(barrier, inc=1, device_id={"sp": (me + hop) % n}, device_id_type=pl.DeviceIdType.MESH)
    fetch_k(0).start()
    for p in range(1, SLOTS):
        fetch_k(p).start()
        fetch_v(p - 1).start()
    fetch_v(SLOTS - 1).start()
    pl.semaphore_wait(barrier, n - 1)

    row = lax.broadcasted_iota(jnp.int32, (2 * heads, LANES), 0) % heads
    lane = lax.broadcasted_iota(jnp.int32, (2 * heads, LANES), 1)
    mine = row // heads_per == lane % key_heads
    diagonal = lax.broadcasted_iota(jnp.int32, (heads, LANES), 0) == lane[:heads]
    diagonal_sums = lax.broadcasted_iota(jnp.int32, (heads, LANES), 0) + SUMS == lane[:heads]

    def twice(ref, slot, tile):
        one = ref[slot, pl.ds(tile * 2 * SIDE, SIDE), :]
        other = ref[slot, pl.ds(tile * 2 * SIDE + SIDE, SIDE), :]
        return jnp.concatenate([one, other], 1)

    def queries(p):
        q = q_ref[seq_of(p)].astype(jnp.float32)
        zero = jnp.zeros_like(q)
        return jnp.concatenate([jnp.concatenate([q, zero], 1), jnp.concatenate([zero, q], 1)], 0).astype(jnp.bfloat16)

    def score_tile(p, both, tile, high):
        s = lax.dot_general(both, twice(kbuf, p % SLOTS, tile), (((1,), (1,)), ((), ())), preferred_element_type=jnp.float32)
        for half in range(SIDE // LANES):
            piece = jnp.where(mine, s[:, half * LANES:(half + 1) * LANES] * factor, -jnp.inf)
            scores[p % 2, tile, :, half * LANES:(half + 1) * LANES] = piece
            high = piece if high is None else jnp.maximum(high, piece)
        return high

    def score_end(p, high):
        high = jnp.maximum(high[:heads], high[heads:])
        highs[p % 2] = jnp.broadcast_to(jnp.max(high, 1, keepdims=True), (heads, LANES))

    def value_tile(p, high, tile, total, seen):
        weights = []
        for half in range(SIDE // LANES):
            w = jnp.exp2(scores[p % 2, tile, :, half * LANES:(half + 1) * LANES] - high)
            total = w if total is None else total + w
            weights.append(w)
        w = jnp.concatenate(weights, 1).astype(jnp.bfloat16)
        add = jnp.dot(w, twice(vbuf, p % SLOTS, tile), preferred_element_type=jnp.float32)
        return total, add if seen is None else seen + add

    def value_end(p, high, total, seen):
        seq = seq_of(p)
        part[seq] = (seen[:heads, :LANES] + seen[heads:, LANES:]).astype(jnp.bfloat16)
        total = jnp.sum(total[:heads] + total[heads:], 1, keepdims=True)
        stat[seq] = jnp.sum(jnp.where(diagonal, high, jnp.where(diagonal_sums, total, 0.0)), 0, keepdims=True)

    def send(p):
        seq = seq_of(p)
        turn = p // n

        @pl.when(p % n < n - 1)
        def _():
            to = {"sp": owner_of(p)}
            pltpu.make_async_remote_copy(part.at[seq], parts.at[turn, me], part_out, part_in.at[turn], device_id=to, device_id_type=pl.DeviceIdType.MESH).start()
            pltpu.make_async_remote_copy(stat.at[seq], stats.at[turn, me], stat_out, stat_in.at[turn], device_id=to, device_id_type=pl.DeviceIdType.MESH).start()

        @pl.when(p % n == n - 1)
        def _():
            parts[turn, me] = part[seq]
            stats[turn, me] = stat[seq]

    def together(turn):
        pltpu.make_async_copy(parts.at[turn, pl.ds(0, n - 1)], parts.at[turn, pl.ds(0, n - 1)], part_in.at[turn]).wait()
        pltpu.make_async_copy(stats.at[turn, pl.ds(0, n - 1)], stats.at[turn, pl.ds(0, n - 1)], stat_in.at[turn]).wait()
        known = stats[turn].reshape(n, LANES)
        scale = jnp.exp2(known - jnp.max(known, 0, keepdims=True))
        sums = pltpu.roll(known, LANES - SUMS, 1)
        scale = scale / jnp.sum(scale * sums, 0, keepdims=True)
        result = None
        for device in range(n):
            own = jnp.sum(jnp.where(diagonal, jnp.broadcast_to(scale[device:device + 1], (heads, LANES)), 0.0), 1, keepdims=True)
            term = parts[turn, device].astype(jnp.float32) * own
            result = term if result is None else result + term
        seq = turn * n + me
        out_ref[seq] = result.astype(out_ref.dtype)
        for hop in range(1, n):
            to = {"sp": (me + (n // 2 + (1 - 2 * (hop % 2)) * (hop // 2) + n) % n) % n}
            pltpu.make_async_remote_copy(out_ref.at[seq], out_ref.at[seq], res_out, res_in, device_id=to, device_id_type=pl.DeviceIdType.MESH).start()

    fetch_k(0).wait()
    both = queries(0)
    high = None
    for tile in range(tiles):
        high = score_tile(0, both, tile, high)
    score_end(0, high)
    if batch > SLOTS:
        fetch_k(SLOTS).start()

    def step(p, _):
        fetch_k(p).wait()
        fetch_v(p - 1).wait()
        both = queries(p)
        last = highs[(p - 1) % 2]
        last_twice = jnp.concatenate([last, last], 0)
        high = total = seen = None
        for tile in range(tiles):
            high = score_tile(p, both, tile, high)
            total, seen = value_tile(p - 1, last_twice, tile, total, seen)
        score_end(p, high)
        value_end(p - 1, last, total, seen)

        @pl.when(p + SLOTS < batch)
        def _():
            fetch_k(p + SLOTS).start()

        @pl.when(p - 1 + SLOTS < batch)
        def _():
            fetch_v(p - 1 + SLOTS).start()

        send(p - 1)

        @pl.when((p > n) & (p % n == n // 2))
        def _():
            together(p // n - 1)

        return 0

    lax.fori_loop(1, batch, step, 0)
    fetch_v(batch - 1).wait()
    last = highs[(batch - 1) % 2]
    last_twice = jnp.concatenate([last, last], 0)
    total = seen = None
    for tile in range(tiles):
        total, seen = value_tile(batch - 1, last_twice, tile, total, seen)
    value_end(batch - 1, last, total, seen)
    send(batch - 1)
    together(rounds - 1)

    away = batch - rounds
    pltpu.make_async_copy(out_ref.at[pl.ds(0, away)], out_ref.at[pl.ds(0, away)], res_in).wait()
    pltpu.make_async_copy(out_ref.at[pl.ds(0, away)], out_ref.at[pl.ds(0, away)], res_out).wait()
    pltpu.make_async_copy(part.at[pl.ds(0, away)], part.at[pl.ds(0, away)], part_out).wait()
    pltpu.make_async_copy(stat.at[pl.ds(0, away)], stat.at[pl.ds(0, away)], stat_out).wait()


def solution(mesh):
    n = mesh.shape["sp"]

    def step(q, k, v):
        batch, heads, head = q.shape
        tokens, key_heads = k.shape[1:3]
        rows = tokens * key_heads
        rounds = batch // n
        vmem = pltpu.VMEM
        return pl.pallas_call(
            functools.partial(attend, n=n, heads_per=heads // key_heads),
            out_shape=jax.ShapeDtypeStruct(q.shape, q.dtype),
            in_specs=[pl.BlockSpec(memory_space=vmem), pl.BlockSpec(memory_space=pl.ANY), pl.BlockSpec(memory_space=pl.ANY)],
            out_specs=pl.BlockSpec(memory_space=vmem),
            scratch_shapes=[
                vmem((SLOTS, rows, head), k.dtype),
                vmem((SLOTS, rows, head), v.dtype),
                vmem((2, rows // (2 * SIDE), 2 * heads, SIDE), jnp.float32),
                vmem((2, heads, LANES), jnp.float32),
                vmem((batch, heads, head), q.dtype),
                vmem((batch, 1, LANES), jnp.float32),
                vmem((rounds, n, heads, head), q.dtype),
                vmem((rounds, n, 1, LANES), jnp.float32),
                pltpu.SemaphoreType.DMA((SLOTS,)),
                pltpu.SemaphoreType.DMA((SLOTS,)),
                pltpu.SemaphoreType.DMA(()),
                pltpu.SemaphoreType.DMA(()),
                pltpu.SemaphoreType.DMA((rounds,)),
                pltpu.SemaphoreType.DMA((rounds,)),
                pltpu.SemaphoreType.DMA(()),
                pltpu.SemaphoreType.DMA(()),
            ],
            compiler_params=pltpu.CompilerParams(collective_id=0, has_side_effects=True, vmem_limit_bytes=60 * 1024 * 1024),
            name="attend",
        )(q, k.reshape(batch, rows, head), v.reshape(batch, rows, head))

    return jax.shard_map(
        step,
        mesh=mesh,
        in_specs=(P("dp", None, None), P("dp", "sp", None, None), P("dp", "sp", None, None)),
        out_specs=P("dp", None, None),
        check_vma=False,
    )
```

time: 139 us -> 48.4 us (0.35)
  the two profiles are of different devices: /device:TPU:21 before, /device:TPU:22 now
where the time goes in v1:
time: 48.4 us; the launch traced here: 48.3 us
  Pallas kernels  46.7 us (96%)
  local copies, waits for them, and re-layouts  1.62 us (3%)
    pallas_call x1, Pallas kernels, step(): pl.pallas_call(functools.partial(attend, n=n, heads_per=heads // key_head...  46.7 us
    unnamed x1, local copies, waits for them, and re-layouts  1.62 us

profile of v1, /device:TPU:22, one launch (start us, length us, event | category | flops | bytes accessed | tf_op | source)
XLA Modules:
  0.0 48.3 jit_solution(17548492969597125097)
XLA Ops:
  0.0 46.7 %attend.1 = bf16[32,24,128]{2,1,0:T(8,128)(2,1)} custom-call(bf16[32,24,128]{2,1,0:T(8,128)(2,1)} %q_ref.1, bf16[32,4096,128]{2,1,0:T(8,128)(2,1)} %bitcast.2, bf16[32,4096,128]{2,1,0:T(8,128)(2,1)} %bitcast.3), custom_call_target="tpu_custom_call" | custom-call | tf_op jit(solution)/shard_map/attend/pallas_call | solution.py:195
  46.7 1.6 %copy.5 = bf16[32,24,128]{2,1,0:T(8,128)(2,1)} copy(bf16[32,24,128]{2,1,0:T(8,128)(2,1)} %attend.1) | data formatting | bytes 393216
